TPU v7x, 32 devices: a whole 2x2x4 slice. The times are simulated.
32 devices in a mesh: row: 8 (over z, x), col: 4 (over y, core).
Axes of the slice: x: 2, y: 2, z: 4, core: 2. Of those that a mesh axis runs over, the one named last changes fastest.
Arguments:
- front_pivot: float32 [64, 128, 128], P('col', 'row'), may hold values from -256 to 256, as said below
- front_update: float32 [64, 640, 768], P('col', 'row'), may hold values from -12 to 12, as said below
- child_blocks: float32 [64, 2, 512, 512], P('col', None, 'row'), may hold values from -0.5 to 0.5, as said below
- child_map: int32 [64, 2, 512], P('col'), may hold values from -1 to 767, as said below
Outputs:
- lhat: float32 [64, 640, 128], P('col', 'row')
- schur: float32 [64, 640, 640], P('col', 'row')
- negative_share: float32 [], replicated
Inputs may be any that keep to these rules, and one draw needn't show every extreme that they name: `front_pivot`: symmetric in its last two dimensions. With both children's entries added, the pivot block of every front has an LDL^T factorization without pivoting whose pivots have magnitudes 4 to 40. `front_update`: the last 640 columns of each front form a symmetric matrix. `child_blocks`: symmetric in its last two dimensions. child_map[f, c, i] is the row and column of front f's assembled matrix that row and column i of child c go to, or -1 for padding. A child's entries of 0 or more are distinct, come before its padding, and number at least 385, and more than half of 512. Parent row p is held by grid row p // 16 if p < 128, else by (p - 128) // 80. Of the 64 rows i of a child with the same i // 64, at most 16 go to rows held by any one grid row, and every child reaches that bound.
All inputs are finite; a program needn't handle non-finite values.
Results may differ from a plain program's by a relative error of at most 0.0003.
Values sent between devices are 32-bit elements; how exact they have to be, the bound alone decides.
No kernel may reach another device: no remote copies, remote signals or barrier semaphores. Data moves between devices by JAX's collectives and lax.ppermute only.
A program may use at most 64 MiB of HBM per device.

v0:
```python
import jax
import jax.numpy as jnp
from jax import lax
from jax.sharding import PartitionSpec as P

highest = lax.Precision.HIGHEST


def factor(blocks):
    fronts, count = (blocks.shape[0], blocks.shape[-1])
    panel_width = 8
    index = jnp.arange(count, dtype=jnp.int32)

    def panel_step(panel, carry):
        current, lower, pivots = carry
        start = panel * panel_width
        strip = lax.dynamic_slice_in_dim(current, start, panel_width, 2)
        columns = []
        values = []
        for inner in range(panel_width):
            place = start + inner
            leading = lax.dynamic_index_in_dim(strip, place, 1, keepdims=False)
            pivot = leading[:, inner]
            below = index[None, :] > place
            column = strip[:, :, inner]
            multiplier = jnp.where(below, column / pivot[:, None], jnp.zeros_like(column))
            strip = strip - multiplier[:, :, None] * leading[:, None, :]
            columns.append(multiplier)
            values.append(pivot)
        panel_lower = jnp.stack(columns, axis=2)
        panel_pivots = jnp.stack(values, axis=1)
        lower = lax.dynamic_update_slice_in_dim(lower, panel_lower, start, 2)
        pivots = lax.dynamic_update_slice_in_dim(pivots, panel_pivots, start, 1)
        product = jnp.einsum(
            "fiw,fjw->fij", panel_lower * panel_pivots[:, None, :], panel_lower, precision=highest
        )
        later = index >= start + panel_width
        current = current - jnp.where(
            later[:, None] & later[None, :], product, jnp.zeros_like(product)
        )
        return (current, lower, pivots)

    start_state = (blocks, jnp.zeros_like(blocks), jnp.zeros((fronts, count), blocks.dtype))
    current, lower, pivots = lax.fori_loop(0, count // panel_width, panel_step, start_state)
    identity = jnp.eye(count, dtype=blocks.dtype)
    inverse = jax.vmap(
        lambda matrix: jax.scipy.linalg.solve_triangular(
            matrix, identity, lower=True, unit_diagonal=True
        )
    )(lower)
    return (inverse, pivots)


def local(front_pivot, front_update, child_blocks, child_map):
    row_count = lax.axis_size("row")
    my_row = lax.axis_index("row")
    fronts, pivot_rows, pivot_width = front_pivot.shape
    update_rows, width = (front_update.shape[1], front_update.shape[2])
    held, child_width = (child_blocks.shape[2], child_blocks.shape[3])
    capacity = 2 * held // row_count
    slot_count = row_count * capacity
    local_rows = pivot_rows + update_rows
    valid = child_map >= 0
    in_pivot = child_map < pivot_width
    owner = jnp.where(in_pivot, child_map // pivot_rows, (child_map - pivot_width) // update_rows)
    owner = jnp.where(valid, owner, row_count)
    target_row = jnp.where(
        in_pivot, child_map % pivot_rows, pivot_rows + (child_map - pivot_width) % update_rows
    )
    owner_hot = (owner[..., None] == jnp.arange(row_count, dtype=jnp.int32)).astype(jnp.int32)
    blocked = owner_hot.reshape(fronts, 2, row_count, held, row_count)
    earlier = jnp.cumsum(blocked, axis=3) - blocked
    rank = jnp.sum(earlier * blocked, axis=4).reshape(fronts, 2, child_width)
    position = jnp.arange(child_width, dtype=jnp.int32)
    slot = owner * capacity + rank
    arrival = (position // held)[None, None, :] * capacity + rank
    my_slot = lax.dynamic_slice_in_dim(slot, my_row * held, held, 2)
    my_valid = lax.dynamic_slice_in_dim(valid, my_row * held, held, 2)
    slot_range = jnp.arange(slot_count, dtype=jnp.int32)
    packing = (
        (my_slot[:, :, None, :] == slot_range[None, None, :, None]) & my_valid[:, :, None, :]
    ).astype(jnp.float32)
    outgoing = jnp.einsum("fcsq,fcqj->fcsj", packing, child_blocks, precision=highest)
    outgoing = outgoing.reshape(fronts, 2, row_count, capacity, child_width)
    incoming = lax.all_to_all(outgoing, "row", split_axis=2, concat_axis=2, tiled=True)
    incoming = incoming.reshape(fronts, 2, slot_count, child_width)
    mine = valid & (owner == my_row)
    row_hot = (
        (target_row[..., None] == jnp.arange(local_rows, dtype=jnp.int32)) & mine[..., None]
    ).astype(jnp.float32)
    arrival_hot = (arrival[..., None] == slot_range).astype(jnp.float32)
    placing = jnp.einsum("fcil,fcip->fclp", row_hot, arrival_hot, precision=highest)
    placed = jnp.einsum("fclp,fcpq->fclq", placing, incoming, precision=highest)
    column_range = jnp.arange(width, dtype=jnp.int32)

    def place_columns(inputs):
        rows_placed, indices = inputs
        column_hot = (indices[:, :, None] == column_range[None, None, :]).astype(jnp.float32)
        total = jnp.dot(
            rows_placed[0], column_hot[0], precision=highest, preferred_element_type=jnp.float32
        )
        return total + jnp.dot(
            rows_placed[1], column_hot[1], precision=highest, preferred_element_type=jnp.float32
        )

    added = lax.map(place_columns, (placed, child_map))
    pivot_local = front_pivot + added[:, :pivot_rows, :pivot_width]
    update_local = front_update + added[:, pivot_rows:, :]
    coupling = update_local[:, :, :pivot_width]
    trailing = update_local[:, :, pivot_width:]
    own_fronts = lax.all_to_all(pivot_local, "row", split_axis=0, concat_axis=1, tiled=True)
    own_inverse, own_pivots = factor(own_fronts)
    inverse, pivots = (
        lax.all_gather(own_inverse, "row", axis=0, tiled=True),
        lax.all_gather(own_pivots, "row", axis=0, tiled=True),
    )
    lhat = jnp.einsum("fik,fjk->fij", coupling, inverse, precision=highest)
    scaled = lhat / pivots[:, None, :]
    correction = jnp.einsum(
        "fik,fjk->fij", scaled, lax.all_gather(lhat, "row", axis=1, tiled=True), precision=highest
    )
    schur = trailing - correction
    negatives = jnp.sum(jnp.where(pivots < 0.0, 1.0, 0.0).astype(jnp.float32))
    total = lax.psum(negatives, "col")
    negative_share = total / (fronts * lax.axis_size("col") * pivot_width)
    return (lhat, schur, negative_share)


def solution(mesh):
    in_specs = (
        P("col", "row", None),
        P("col", "row", None),
        P("col", None, "row", None),
        P("col", None, None),
    )
    out_specs = (P("col", "row", None), P("col", "row", None), P())
    return jax.shard_map(local, mesh=mesh, in_specs=in_specs, out_specs=out_specs, check_vma=False)
```

profile of v0, /device:TPU:0, one launch (start us, length us, event | category | flops | bytes accessed | tf_op | source)
XLA Modules:
  0.0 599.0 jit_solution(478743614236139514)
XLA Ops:
  8.6 42.6 %fusion.18 = s32[16,2,8,64]{2,3,1,0:T(8,128)S(1)} fusion(s32[16,2,8,64]{2,3,1,0:T(8,128)S(1)} %copy.48), kind=kOutput, calls=%fused_computation.74 | output fusion | flops 9158656 | bytes 131072 | tf_op jit(solution)/shard_map/jit(cumsum)/reduce_window_sum | solution.py:72
  51.8 6.6 %fusion.27 = f32[16,2,128,512]{3,2,1,0:T(8,128)S(1)} fusion(f32[16,2,64,512]{3,2,1,0:T(8,128)} %param.10, s32[16,2,64]{2,1,0:T(2,128)S(1)} %copy.51, pred[16,2,64]{2,1,0:T(4,128)(4,1)S(1)} %copy.52), kind=kOutput, calls=%fused_computation.88 | convolution fusion | flops 1611137024 | bytes 12593152 | tf_op jit(solution)/shard_map/fcsq,fcqj->fcsj/dot_general | solution.py:83
  58.4 4.3 copy.53
  62.7 7.4 %all-to-all-start = ((f32[16,2,8,16,512]{4,3,1,0,2:T(8,128)}), f32[16,2,8,16,512]{4,3,1,0,2:T(8,128)}, u32[]{:S(2)}, u32[]{:S(2)}) async-start(f32[16,2,8,16,512]{4,3,1,0,2:T(8,128)} %copy.53), calls=%async_computation | async-start | bytes 16777216 | tf_op jit(solution)/shard_map/all_to_all | solution.py:85
  70.4 6.0 fusion.19
  76.3 176.9 %all-to-all-done = f32[16,2,8,16,512]{4,3,1,0,2:T(8,128)} async-done(((f32[16,2,8,16,512]{4,3,1,0,2:T(8,128)}), f32[16,2,8,16,512]{4,3,1,0,2:T(8,128)}, u32[]{:S(2)}, u32[]{:S(2)}) %all-to-all-start) | async-done | bytes 8388640 | tf_op jit(solution)/shard_map/all_to_all | solution.py:85
  253.3 4.4 copy.54
  257.7 7.6 %fusion.61 = f32[16,2,96,512]{3,2,1,0:T(8,128)} fusion(f32[16,2,96,128]{3,2,1,0:T(8,128)S(1)} %fusion.19, f32[16,2,128,512]{3,2,1,0:T(8,128)S(1)} %bitcast.85), kind=kOutput, calls=%fused_computation.148 | convolution fusion | flops 2415919104 | bytes 16252928 | tf_op jit(solution)/shard_map/fclp,fcpq->fclq/dot_general | solution.py:93
  265.3 69.4 %while.33 = (s32[]{:T(128)}, f32[16,96,768]{2,1,0:T(8,128)}, f32[16,2,96,512]{3,2,1,0:T(8,128)}, s32[16,2,512]{2,1,0:T(2,128)S(1)}, s32[]{:T(128)}, /*index=5*/s32[]{:T(128)}, s32[]{}) while((s32[]{:T(128)}, f32[16,96,768]{2,1,0:T(8,128)}, f32[16,2,96,512]{3,2,1,0:T(8,128)}, s32[16,2,512]{2,1,0:T(2,128)S(1)}, s32[]{:T(128)}, ...), condition=%wide.region_3.4_spmd.clone, body=%wide.region_2.3_spmd.clone.sunk | while | flops 906829824 | bytes 2864737 | solution.py:106
  267.4 2.3 fusion.82
  270.1 1.6 fusion.81
  271.7 2.3 fusion.82
  274.5 1.6 fusion.81
  276.0 2.3 fusion.82
  278.8 1.6 fusion.81
  280.3 2.3 fusion.82
  283.1 1.6 fusion.81
  284.7 2.3 fusion.82
  287.4 1.6 fusion.81
  289.0 2.3 fusion.82
  291.8 1.6 fusion.81
  293.3 2.3 fusion.82
  296.1 1.6 fusion.81
  297.7 2.3 fusion.82
  300.5 1.6 fusion.81
  302.0 2.3 fusion.82
  306.4 2.3 fusion.82
  309.2 1.6 fusion.81
  310.7 2.3 fusion.82
  315.1 2.3 fusion.82
  319.4 2.3 fusion.82
  323.7 2.3 fusion.82
  326.5 1.6 fusion.81
  328.1 2.2 fusion.82
  330.8 1.6 fusion.81
  332.4 2.3 fusion.82
  334.7 1.6 slice_add_fusion.1
  336.2 3.6 all-to-all-start.1
  340.0 7.2 %all-to-all-done.1 = f32[16,16,128]{2,1,0:T(8,128)S(1)} async-done(((f32[16,16,128]{2,1,0:T(8,128)}), f32[16,16,128]{2,1,0:T(8,128)S(1)}, u32[]{:S(2)}, u32[]{:S(2)}) %all-to-all-start.1) | async-done | bytes 131104 | tf_op jit(solution)/shard_map/all_to_all | solution.py:111
  347.4 83.5 %while.34 = (s32[]{:T(128)}, f32[2,128,128]{1,2,0:T(8,128)S(1)}, f32[2,128,128]{1,2,0:T(8,128)S(1)}, f32[2,128]{1,0:T(2,128)S(1)}, s32[]{:T(128)}, /*index=5*/s3...) while((s32[]{:T(128)}, f32[2,128,128]{1,2,0:T(8,128)S(1)}, ...), condition=%wide.region_5.6_spmd.clone.clone, body=%wide.region_4.5_spmd.clone.clone.sunk | while | flops 3349669 | bytes 1026329 | solution.py:44
  431.0 19.7 %custom-call.4 = f32[2,1,128,128]{2,3,1,0:T(8,128)S(1)} custom-call(f32[2,1,128,128]{3,2,1,0:T(8,128)S(1)} %add_bitcast_fusion), custom_call_target="InvertDiagBlocksLowerTriangular" | custom-call | tf_op jit(solution)/shard_map/vmap(jit(_solve_triangular))/triangular_solve | solution.py:47
  452.0 5.8 slice_add_fusion
  457.8 32.4 %all-gather.4.cloned.1.call-done = f32[16,128,128]{2,1,0:T(8,128)} async-done(((f32[2,128,128]{2,1,0:T(8,128)}), f32[16,128,128]{2,1,0:T(8,128)}) %all-gather.4.cloned.1.call-update) | async-done | bytes 1048592 | tf_op jit(solution)/shard_map/all_gather | solution.py:114
  490.1 4.4 fusion.29
  494.6 18.7 %all-gather = f32[8,2,128]{2,1,0:T(2,128)S(1)} all-gather(f32[1,2,128]{2,1,0:T(2,128)S(1)} %bitcast.118), channel_id=1, replica_groups=mesh['row'=8,'col'=4] {'row'}, dimensions={0}, use_global_device_ids=true | all-gather | bytes 9216 | tf_op jit(solution)/shard_map/all_gather | solution.py:115
  513.9 6.7 %psum.7 = f32[]{:T(128)} all-reduce(f32[]{:T(128)} %select_reduce_fusion), channel_id=1, replica_groups=mesh['row'=8,'col'=4] {'col'}, use_global_device_ids=true, to_apply=%region_7.8 | all-reduce | flops 1 | bytes 8 | tf_op jit(solution)/shard_map/psum | solution.py:124
  521.2 58.1 %all-gather.6.cloned.1.call-done = f32[16,640,128]{2,1,0:T(8,128)} async-done(((f32[16,80,128]{2,1,0:T(8,128)}), f32[16,640,128]{2,1,0:T(8,128)}) %all-gather.6.cloned.1.call-update) | async-done | bytes 5242896 | tf_op jit(solution)/shard_map/all_gather | solution.py:120
  579.4 11.6 %slice_subtract_fusion = f32[16,80,640]{2,1,0:T(8,128)} fusion(f32[16,80,768]{2,1,0:T(8,128)} %slice_add_fusion, f32[16,640,128]{2,1,0:T(8,128)} %all-gather.6.cloned.1.call-done, f32[16,80,128]{2,1,0:T(8,128)} %fusion.29, f32[16,128]{1,0:T(8,128)S(1)} %bitcast.117), kind=kOutput, calls=%fused_computation.83 | convolution fusion | flops 1259274240 | bytes 12460032 | tf_op jit(solution)/shard_map/fik,fjk->fij/dot_general | solution.py:119
  (840 shorter events, 100.9 us)
Async XLA Ops:
  62.7 7.5 %copy-start = (s32[16,2,512]{2,1,0:T(2,128)S(1)}, s32[16,2,512]{2,1,0:T(2,128)}, u32[]{:S(2)}) copy-start(s32[16,2,512]{2,1,0:T(2,128)} %param.11) | copy-start | bytes 196612
  62.7 190.6 %all-to-all-start = ((f32[16,2,8,16,512]{4,3,1,0,2:T(8,128)}), f32[16,2,8,16,512]{4,3,1,0,2:T(8,128)}, u32[]{:S(2)}, u32[]{:S(2)}) async-start(f32[16,2,8,16,512]{4,3,1,0,2:T(8,128)} %copy.53), calls=%async_computation | async-start | bytes 16777216 | tf_op jit(solution)/shard_map/all_to_all | solution.py:85
  265.3 69.4 %copy-start.1 = (f32[16,16,128]{2,1,0:T(8,128)S(1)}, f32[16,16,128]{2,1,0:T(8,128)}, u32[]{:S(2)}) copy-start(f32[16,16,128]{2,1,0:T(8,128)} %param.8) | copy-start | bytes 393220
  336.2 11.0 %all-to-all-start.1 = ((f32[16,16,128]{2,1,0:T(8,128)}), f32[16,16,128]{2,1,0:T(8,128)S(1)}, u32[]{:S(2)}, u32[]{:S(2)}) async-start(f32[16,16,128]{2,1,0:T(8,128)} %slice_add_fusion.1), calls=%async_computation.1 | async-start | bytes 262144 | tf_op jit(solution)/shard_map/all_to_all | solution.py:111
  339.9 150.3 %all-gather.4.cloned.1.call-start = ((), (), s32[]{:S(2)}) async-start(), calls=%async_computation.2 | async-start | bytes 1179648 | tf_op jit(solution)/shard_map/all_gather | solution.py:114
  451.7 127.7 %all-gather.6.cloned.1.call-start = ((), (), s32[]{:S(2)}) async-start(), calls=%async_computation.3 | async-start | bytes 5898240 | tf_op jit(solution)/shard_map/all_gather | solution.py:120
Sparse Core Ops, SparseCore 0:
  451.8 38.2 all-gather.3
  494.7 84.6 all-gather.5
where the time goes:
time: 600 us; the launch traced here: 599 us
  waiting for transfers between devices  275 us (46%)
  matrix products  106 us (18%)
  other arithmetic  101 us (17%)
  local copies, waits for them, and re-layouts  62.1 us (10%)
  blocking collectives  25.4 us (4%)
  between operations  16 us (3%)
  starting transfers between devices  11.3 us (2%)
    all_to_all x1, waiting for transfers between devices, local(): lax.all_to_all(outgoing, 'row', split_axis=2, concat_axis=2, tiled=True)  177 us
    all_gather x1, waiting for transfers between devices, local(): lax.all_gather(lhat, 'row', axis=1, tiled=True)  58.1 us
    another operation x1, other arithmetic, local(): earlier = jnp.cumsum(blocked, axis=3) - blocked  42.6 us
    dot_general x16, matrix products, place_columns(): jnp.dot(rows_placed[0], column_hot[0], precision=highest, preferred_eleme...  36.3 us
    all_gather x1, waiting for transfers between devices, local(): lax.all_gather(own_inverse, 'row', axis=0, tiled=True)  32.4 us
    dot_general x16, matrix products, place_columns(): jnp.dot(rows_placed[1], column_hot[1], precision=highest, preferred_eleme...  24.8 us
    slice x128, local copies, waits for them, and re-layouts, panel_step(): pivot = leading[:, inner]  22.7 us
    dynamic_slice x128, local copies, waits for them, and re-layouts, panel_step(): leading = lax.dynamic_index_in_dim(strip, place, 1, keepdims=False)  20.2 us
  transfers between devices with their start and end apart: 4, of which 4 were waited for; matrix products, arithmetic and copies ran while one was open for 2% of the time, Pallas kernels for 0%

commit v1 on v0

--- a/solution.py
+++ b/solution.py
@@ -82,7 +82,10 @@
     ).astype(jnp.float32)
     outgoing = jnp.einsum("fcsq,fcqj->fcsj", packing, child_blocks, precision=highest)
     outgoing = outgoing.reshape(fronts, 2, row_count, capacity, child_width)
-    incoming = lax.all_to_all(outgoing, "row", split_axis=2, concat_axis=2, tiled=True)
+    incoming = jnp.concatenate(
+        lax.all_to_all(jnp.stack(jnp.split(outgoing, lax.axis_size("row"), axis=2)), "row", 0, 0),
+        axis=2,
+    )
     incoming = incoming.reshape(fronts, 2, slot_count, child_width)
     mine = valid & (owner == my_row)
     row_hot = (

time: 600 us -> 604 us (level)
    unnamed x5 -> x12, local copies, waits for them, and re-layouts: 0.1 us -> 7.63 us
where the time goes in v1:
time: 604 us; the launch traced here: 603 us
  waiting for transfers between devices  275 us (46%)
  matrix products  106 us (18%)
  other arithmetic  101 us (17%)
  local copies, waits for them, and re-layouts  66.4 us (11%)
  blocking collectives  25.4 us (4%)
  between operations  16 us (3%)
  starting transfers between devices  11.3 us (2%)
    all_to_all x1, waiting for transfers between devices, local(): lax.all_to_all(jnp.stack(jnp.split(outgoing, lax.axis_size('row'), axis=2...  177 us
    all_gather x1, waiting for transfers between devices, local(): lax.all_gather(lhat, 'row', axis=1, tiled=True)  58.1 us
    another operation x1, other arithmetic, local(): earlier = jnp.cumsum(blocked, axis=3) - blocked  42.6 us
    dot_general x16, matrix products, place_columns(): jnp.dot(rows_placed[0], column_hot[0], precision=highest, preferred_eleme...  36.3 us
    all_gather x1, waiting for transfers between devices, local(): lax.all_gather(own_inverse, 'row', axis=0, tiled=True)  32.6 us
    dot_general x16, matrix products, place_columns(): jnp.dot(rows_placed[1], column_hot[1], precision=highest, preferred_eleme...  24.8 us
    slice x128, local copies, waits for them, and re-layouts, panel_step(): pivot = leading[:, inner]  22.7 us
    dynamic_slice x128, local copies, waits for them, and re-layouts, panel_step(): leading = lax.dynamic_index_in_dim(strip, place, 1, keepdims=False)  20.2 us
  transfers between devices with their start and end apart: 4, of which 4 were waited for; matrix products, arithmetic and copies ran while one was open for 2% of the time, Pallas kernels for 0%

profile of v1, /device:TPU:0, one launch (start us, length us, event | category | flops | bytes accessed | tf_op | source)
XLA Modules:
  0.0 603.1 jit_solution(8654890875188140657)
XLA Ops:
  8.6 42.6 %fusion.18 = s32[16,2,8,64]{2,3,1,0:T(8,128)S(1)} fusion(s32[16,2,8,64]{2,3,1,0:T(8,128)S(1)} %copy.78), kind=kOutput, calls=%fused_computation.74 | output fusion | flops 9158656 | bytes 131072 | tf_op jit(solution)/shard_map/jit(cumsum)/reduce_window_sum | solution.py:72
  51.8 6.4 %fusion.35 = f32[16,2,128,512]{3,2,1,0:T(8,128)S(1)} fusion(f32[16,2,64,512]{3,2,1,0:T(8,128)} %param.10, s32[16,2,64]{2,1,0:T(2,128)S(1)} %copy.81, pred[16,2,64]{2,1,0:T(4,128)(4,1)S(1)} %copy.82), kind=kOutput, calls=%fused_computation.104 | convolution fusion | flops 1611137024 | bytes 12593152 | tf_op jit(solution)/shard_map/fcsq,fcqj->fcsj/dot_general | solution.py:83
  66.8 7.4 %all-to-all-start = ((f32[8,16,2,1,16,512]{5,4,2,1,3,0:T(8,128)}), f32[8,16,2,1,16,512]{5,4,2,1,3,0:T(8,128)}, u32[]{:S(2)}, u32[]{:S(2)}) async-start(f32[8,16,2,1,16,512]{5,4,2,1,3,0:T(8,128)} %fusion.26), calls=%async_computation | async-start | bytes 16777216 | tf_op jit(solution)/shard_map/all_to_all | solution.py:86
  74.5 6.0 fusion.19
  80.5 176.9 %all-to-all-done = f32[8,16,2,1,16,512]{5,4,2,1,3,0:T(8,128)} async-done(((f32[8,16,2,1,16,512]{5,4,2,1,3,0:T(8,128)}), f32[8,16,2,1,16,512]{5,4,2,1,3,0:T(8,128)}, u32[]{:S(2)}, u32[]{:S(2)}) %all-to-all-start) | async-done | bytes 8388640 | tf_op jit(solution)/shard_map/all_to_all | solution.py:86
  257.4 4.4 copy.90
  261.9 7.6 %fusion.69 = f32[16,2,96,512]{3,2,1,0:T(8,128)} fusion(f32[16,2,96,128]{3,2,1,0:T(8,128)S(1)} %fusion.19, f32[16,2,128,512]{3,2,1,0:T(8,128)S(1)} %bitcast.139), kind=kOutput, calls=%fused_computation.164 | convolution fusion | flops 2415919104 | bytes 16252928 | tf_op jit(solution)/shard_map/fclp,fcpq->fclq/dot_general | solution.py:96
  269.5 69.4 %while.33 = (s32[]{:T(128)}, f32[16,96,768]{2,1,0:T(8,128)}, f32[16,2,96,512]{3,2,1,0:T(8,128)}, s32[16,2,512]{2,1,0:T(2,128)S(1)}, s32[]{:T(128)}, /*index=5*/s32[]{:T(128)}, s32[]{}) while((s32[]{:T(128)}, f32[16,96,768]{2,1,0:T(8,128)}, f32[16,2,96,512]{3,2,1,0:T(8,128)}, s32[16,2,512]{2,1,0:T(2,128)S(1)}, s32[]{:T(128)}, ...), condition=%wide.region_3.4_spmd.clone, body=%wide.region_2.3_spmd.clone.sunk | while | flops 906829824 | bytes 2864737 | solution.py:109
  271.5 2.3 fusion.90
  274.3 1.6 fusion.89
  275.9 2.3 fusion.90
  278.6 1.6 fusion.89
  280.2 2.3 fusion.90
  283.0 1.6 fusion.89
  284.5 2.3 fusion.90
  287.3 1.6 fusion.89
  288.8 2.3 fusion.90
  291.6 1.6 fusion.89
  293.2 2.3 fusion.90
  296.0 1.6 fusion.89
  297.5 2.3 fusion.90
  300.3 1.6 fusion.89
  301.9 2.3 fusion.90
  304.7 1.6 fusion.89
  306.2 2.3 fusion.90
  310.6 2.3 fusion.90
  313.3 1.6 fusion.89
  314.9 2.3 fusion.90
  317.7 1.6 fusion.89
  319.2 2.3 fusion.90
  323.6 2.3 fusion.90
  327.9 2.3 fusion.90
  330.7 1.6 fusion.89
  332.2 2.2 fusion.90
  335.0 1.6 fusion.89
  336.6 2.3 fusion.90
  338.8 1.6 slice_add_fusion.1
  340.4 3.6 all-to-all-start.1
  344.4 7.0 %all-to-all-done.1 = f32[16,16,128]{2,1,0:T(8,128)S(1)} async-done(((f32[16,16,128]{2,1,0:T(8,128)}), f32[16,16,128]{2,1,0:T(8,128)S(1)}, u32[]{:S(2)}, u32[]{:S(2)}) %all-to-all-start.1) | async-done | bytes 131104 | tf_op jit(solution)/shard_map/all_to_all | solution.py:114
  351.5 83.5 %while.34 = (s32[]{:T(128)}, f32[2,128,128]{1,2,0:T(8,128)S(1)}, f32[2,128,128]{1,2,0:T(8,128)S(1)}, f32[2,128]{1,0:T(2,128)S(1)}, s32[]{:T(128)}, /*index=5*/s3...) while((s32[]{:T(128)}, f32[2,128,128]{1,2,0:T(8,128)S(1)}, ...), condition=%wide.region_5.6_spmd.clone.clone, body=%wide.region_4.5_spmd.clone.clone.sunk | while | flops 3349669 | bytes 1026329 | solution.py:44
  435.1 19.7 %custom-call.4 = f32[2,1,128,128]{2,3,1,0:T(8,128)S(1)} custom-call(f32[2,1,128,128]{3,2,1,0:T(8,128)S(1)} %add_bitcast_fusion), custom_call_target="InvertDiagBlocksLowerTriangular" | custom-call | tf_op jit(solution)/shard_map/vmap(jit(_solve_triangular))/triangular_solve | solution.py:47
  455.9 5.8 slice_add_fusion
  461.7 32.6 %all-gather.4.cloned.1.call-done = f32[16,128,128]{2,1,0:T(8,128)} async-done(((f32[2,128,128]{2,1,0:T(8,128)}), f32[16,128,128]{2,1,0:T(8,128)}) %all-gather.4.cloned.1.call-update) | async-done | bytes 1048592 | tf_op jit(solution)/shard_map/all_gather | solution.py:117
  494.3 4.4 fusion.37
  498.8 18.7 %all-gather = f32[8,2,128]{2,1,0:T(2,128)S(1)} all-gather(f32[1,2,128]{2,1,0:T(2,128)S(1)} %bitcast.172), channel_id=1, replica_groups=mesh['row'=8,'col'=4] {'row'}, dimensions={0}, use_global_device_ids=true | all-gather | bytes 9216 | tf_op jit(solution)/shard_map/all_gather | solution.py:118
  518.1 6.7 %psum.7 = f32[]{:T(128)} all-reduce(f32[]{:T(128)} %select_reduce_fusion), channel_id=1, replica_groups=mesh['row'=8,'col'=4] {'col'}, use_global_device_ids=true, to_apply=%region_7.8 | all-reduce | flops 1 | bytes 8 | tf_op jit(solution)/shard_map/psum | solution.py:127
  525.4 58.1 %all-gather.6.cloned.1.call-done = f32[16,640,128]{2,1,0:T(8,128)} async-done(((f32[16,80,128]{2,1,0:T(8,128)}), f32[16,640,128]{2,1,0:T(8,128)}) %all-gather.6.cloned.1.call-update) | async-done | bytes 5242896 | tf_op jit(solution)/shard_map/all_gather | solution.py:123
  583.5 11.6 %slice_subtract_fusion = f32[16,80,640]{2,1,0:T(8,128)} fusion(f32[16,80,768]{2,1,0:T(8,128)} %slice_add_fusion, f32[16,640,128]{2,1,0:T(8,128)} %all-gather.6.cloned.1.call-done, f32[16,80,128]{2,1,0:T(8,128)} %fusion.37, f32[16,128]{1,0:T(8,128)S(1)} %bitcast.171), kind=kOutput, calls=%fused_computation.83 | convolution fusion | flops 1259274240 | bytes 12460032 | tf_op jit(solution)/shard_map/fik,fjk->fij/dot_general | solution.py:122
  (847 shorter events, 107.9 us)
Async XLA Ops:
  66.8 7.5 %copy-start = (s32[16,2,512]{2,1,0:T(2,128)S(1)}, s32[16,2,512]{2,1,0:T(2,128)}, u32[]{:S(2)}) copy-start(s32[16,2,512]{2,1,0:T(2,128)} %param.11) | copy-start | bytes 196612
  66.8 190.6 %all-to-all-start = ((f32[8,16,2,1,16,512]{5,4,2,1,3,0:T(8,128)}), f32[8,16,2,1,16,512]{5,4,2,1,3,0:T(8,128)}, u32[]{:S(2)}, u32[]{:S(2)}) async-start(f32[8,16,2,1,16,512]{5,4,2,1,3,0:T(8,128)} %fusion.26), calls=%async_computation | async-start | bytes 16777216 | tf_op jit(solution)/shard_map/all_to_all | solution.py:86
  269.4 69.4 %copy-start.1 = (f32[16,16,128]{2,1,0:T(8,128)S(1)}, f32[16,16,128]{2,1,0:T(8,128)}, u32[]{:S(2)}) copy-start(f32[16,16,128]{2,1,0:T(8,128)} %param.8) | copy-start | bytes 393220
  340.4 11.0 %all-to-all-start.1 = ((f32[16,16,128]{2,1,0:T(8,128)}), f32[16,16,128]{2,1,0:T(8,128)S(1)}, u32[]{:S(2)}, u32[]{:S(2)}) async-start(f32[16,16,128]{2,1,0:T(8,128)} %slice_add_fusion.1), calls=%async_computation.1 | async-start | bytes 262144 | tf_op jit(solution)/shard_map/all_to_all | solution.py:114
  344.0 150.3 %all-gather.4.cloned.1.call-start = ((), (), s32[]{:S(2)}) async-start(), calls=%async_computation.2 | async-start | bytes 1179648 | tf_op jit(solution)/shard_map/all_gather | solution.py:117
  455.9 127.7 %all-gather.6.cloned.1.call-start = ((), (), s32[]{:S(2)}) async-start(), calls=%async_computation.3 | async-start | bytes 5898240 | tf_op jit(solution)/shard_map/all_gather | solution.py:123
Sparse Core Ops, SparseCore 0:
  456.0 38.2 all-gather.3
  498.9 84.6 all-gather.5
